TPU v7x, 32 devices: a whole 2x2x4 slice. The times are simulated.
32 devices in a mesh: pa: 16 (over z, y, core), pb: 2 (over x).
Axes of the slice: x: 2, y: 2, z: 4, core: 2. Of those that a mesh axis runs over, the one named last changes fastest.
Arguments:
- sources: float32 [4096, 128], P(('pa', 'pb')), may hold values from -3 to 3, as said below
- targets: bfloat16 [4096, 128], P(('pa', 'pb')), may hold values from -2 to 2, as said below
- source_mass: float32 [4096], P(('pa', 'pb')), may hold values from -1 to 1
- target_mass: float32 [4096], P(('pa', 'pb')), may hold values from -1 to 1
Outputs:
- moved: float32 [4096, 128], P(('pa', 'pb'))
- dual_source: float32 [4096], P(('pa', 'pb'))
- dual_target: float32 [4096], P(('pa', 'pb'))
Inputs may be any that keep to these rules, and one draw needn't show every extreme that they name: `targets`: each block of 128 target rows is drawn around one cluster centre, a different one for each block. `sources`: each block of 128 source rows is drawn around a cluster centre of its own, drawn independently of the target centres, possibly offset by a common shift.
All inputs are finite; a program needn't handle non-finite values.
Results may differ from a plain program's by a relative error of at most 0.003.
Values may be sent and summed in bfloat16 or wider, within the bound.
A program may use at most 64 MiB of HBM per device.

v0:
```python
from functools import partial

import jax
import jax.numpy as jnp
from jax import lax
from jax.sharding import PartitionSpec as P

STEPS = 1
ITERS = 2


step_rate = 0.25
floor_value = -1e30


def merged(part, axis, combine):
    gathered = jax.tree.map(lambda a: lax.all_gather(a, axis), part)

    def take(source):
        return jax.tree.map(lambda a: lax.dynamic_index_in_dim(a, source, 0, False), gathered)

    return lax.fori_loop(
        1, lax.axis_size(axis), lambda source, state: combine(state, take(source)), take(0)
    )


def squares(coords):
    wide = coords.astype(jnp.float32)
    return jnp.sum(wide * wide, axis=1)


def pair_cost(left, left_norm, right, right_norm):
    inner = lax.dot_general(
        left, right, (((1,), (1,)), ((), ())), preferred_element_type=jnp.float32
    )
    return left_norm[:, None] + right_norm[None, :] - 2.0 * inner


def over_blocks(update, carry, total):
    block_width = 512 if total % 512 == 0 else total
    block_count = total // block_width
    if block_count == 1:
        return update(carry, 0, block_width)
    return lax.fori_loop(
        0,
        block_count,
        lambda position, current: update(current, position * block_width, block_width),
        carry,
    )


def lse_piece(rows, row_norm, columns, column_norm, carry, piece, start):

    def update(current, offset, length):
        chosen = lax.dynamic_slice_in_dim(columns, start + offset, length, 0)
        chosen_norm = lax.dynamic_slice_in_dim(column_norm, start + offset, length, 0)
        values = lax.dynamic_slice_in_dim(piece, offset, length, 0)
        scores = values[None, :] - pair_cost(rows, row_norm, chosen, chosen_norm)
        highest, totals = current
        raised = jnp.maximum(highest, jnp.max(scores, axis=1))
        totals = totals * jnp.exp(highest - raised) + jnp.sum(
            jnp.exp(scores - raised[:, None]), axis=1
        )
        return (raised, totals)

    return over_blocks(update, carry, piece.shape[0])


def plan_piece(rows, row_norm, row_pot, columns, column_norm, carry, piece, start):

    def update(current, offset, length):
        chosen = lax.dynamic_slice_in_dim(columns, start + offset, length, 0)
        chosen_norm = lax.dynamic_slice_in_dim(column_norm, start + offset, length, 0)
        values = lax.dynamic_slice_in_dim(piece, offset, length, 0)
        cost = pair_cost(rows, row_norm, chosen, chosen_norm)
        weights = jnp.exp(row_pot[:, None] + values[None, :] - cost).astype(jnp.bfloat16)
        return current + jnp.dot(weights, chosen, preferred_element_type=jnp.float32)

    return over_blocks(update, carry, piece.shape[0])


def join_lse(first, second):
    raised = jnp.maximum(first[0], second[0])
    return (raised, first[1] * jnp.exp(first[0] - raised) + second[1] * jnp.exp(second[0] - raised))


def start_lse(length):
    return (jnp.full((length,), floor_value, jnp.float32), jnp.zeros((length,), jnp.float32))


def finish(carry):
    return -(carry[0] + jnp.log(carry[1]))


def body(sources, targets, source_mass, target_mass):
    own_rows = sources.shape[0]
    own_targets = targets.shape[0]
    target_norm = squares(targets)
    moving = sources
    dual_target = jnp.zeros((own_targets,), jnp.float32)
    dual_source = jnp.zeros((own_rows,), jnp.float32)
    member = lax.axis_index("pb")
    half_targets = lax.all_gather(targets, "pa", axis=0, tiled=True)
    half_norm = squares(half_targets)
    pair_mass = lax.all_gather(source_mass, "pb", axis=0, tiled=True)
    pair_dual = jnp.zeros((pair_mass.shape[0],), jnp.float32)
    for flow_step in range(STEPS):
        coarse = moving.astype(jnp.bfloat16)
        pair_coarse = lax.all_gather(coarse, "pb", axis=0, tiled=True)
        pair_norm = squares(pair_coarse)
        pair_count = pair_coarse.shape[0]
        all_sources = lax.all_gather(pair_coarse, "pa", axis=0, tiled=True)
        all_source_norm = squares(all_sources)
        row_fold = partial(lse_piece, pair_coarse, pair_norm, half_targets, half_norm)
        column_fold = partial(lse_piece, targets, target_norm, all_sources, all_source_norm)
        shifted = dual_target + target_mass
        for sweep in range(ITERS + 1):
            shifted = dual_target + target_mass
            half_lse = row_fold(
                start_lse(pair_count),
                jax.tree.map(lambda part: lax.all_gather(part, "pa", axis=0, tiled=True), shifted),
                jnp.int32(0),
            )
            pair_dual = finish(merged((half_lse[0], half_lse[1]), "pb", join_lse))
            if sweep < ITERS:
                lifted = pair_dual + pair_mass
                dual_target = finish(
                    column_fold(
                        start_lse(own_targets),
                        jax.tree.map(
                            lambda part: lax.all_gather(part, "pa", axis=0, tiled=True), lifted
                        ),
                        jnp.int32(0),
                    )
                )
        plan_fold = partial(plan_piece, pair_coarse, pair_norm, pair_dual, half_targets, half_norm)
        empty = jnp.zeros((pair_count, sources.shape[1]), jnp.float32)
        pair_centre = plan_fold(
            empty,
            jax.tree.map(lambda part: lax.all_gather(part, "pa", axis=0, tiled=True), shifted),
            jnp.int32(0),
        )
        centre = lax.psum_scatter(
            pair_centre.astype(jnp.bfloat16), "pb", scatter_dimension=0, tiled=True
        ).astype(jnp.float32)
        moving = moving - 2.0 * step_rate * (moving - centre)
    dual_source = lax.dynamic_slice_in_dim(pair_dual, member * own_rows, own_rows, 0)
    return (moving, dual_source, dual_target)


def solution(mesh):
    return jax.shard_map(
        body,
        mesh=mesh,
        in_specs=(P(("pa", "pb"), None), P(("pa", "pb"), None), P(("pa", "pb")), P(("pa", "pb"))),
        out_specs=(P(("pa", "pb"), None), P(("pa", "pb")), P(("pa", "pb"))),
        check_vma=False,
    )
```

profile of v0, /device:TPU:0, one launch (start us, length us, event | category | flops | bytes accessed | tf_op | source)
XLA Modules:
  0.0 212.1 jit_solution(4313513718906820735)
XLA Ops:
  8.1 5.6 %all_gather.65 = bf16[256,128]{1,0:T(8,128)(2,1)} all-gather(bf16[128,128]{1,0:T(8,128)(2,1)S(1)} %convert_element_type.28), channel_id=1, replica_groups=mesh['pa'=16,'pb'=2] {'pb'}, dimensions={0}, use_global_device_ids=true | all-gather | bytes 98304 | tf_op jit(solution)/shard_map/all_gather | solution.py:109
  14.8 24.3 %all_gather.66 = bf16[2048,128]{1,0:T(8,128)(2,1)S(1)} all-gather(bf16[128,128]{1,0:T(8,128)(2,1)} %param.17), channel_id=1, replica_groups=mesh['pa'=16,'pb'=2] {'pa'}, dimensions={0}, use_global_device_ids=true | all-gather | bytes 557056 | tf_op jit(solution)/shard_map/all_gather | solution.py:103
  39.4 17.5 %all-gather.6 = f32[16,1,128]{2,1,0:T(1,128)S(1)} all-gather(f32[1,1,128]{2,1,0:T(1,128)S(1)} %bitcast.107), channel_id=1, replica_groups=mesh['pa'=16,'pb'=2] {'pa'}, dimensions={0}, use_global_device_ids=true | all-gather | bytes 8704 | tf_op jit(solution)/shard_map/all_gather | solution.py:121
  56.9 2.4 %while.112 = (s32[]{:T(128)}, f32[256]{0:T(256)S(1)}, f32[256]{0:T(256)S(1)}, f32[2048]{0:T(1024)S(1)}, f32[256]{0:T(256)S(1)}, /*index=5*/f32[2048]{0:T(1024)S(...) while((s32[]{:T(128)}, f32[256]{0:T(256)S(1)}, ...), condition=%wide.region_6.7_spmd.clone, body=%wide.region_3.6_spmd.clone.sunk | while | flops 34473220 | bytes 1271994 | solution.py:44
  59.5 4.2 %all-gather.9 = f32[2,1,128]{2,1,0:T(1,128)S(1)} all-gather(f32[1,1,128]{2,1,0:T(1,128)S(1)} %bitcast.124), channel_id=1, replica_groups=mesh['pa'=16,'pb'=2] {'pb'}, dimensions={0}, use_global_device_ids=true | all-gather | bytes 1536 | tf_op jit(solution)/shard_map/all_gather | solution.py:105
  63.7 4.2 %all-gather.7 = f32[2,1,256]{2,1,0:T(1,128)S(1)} all-gather(f32[1,1,256]{2,1,0:T(1,128)S(1)} %bitcast.98), channel_id=2, replica_groups=mesh['pa'=16,'pb'=2] {'pb'}, dimensions={0}, use_global_device_ids=true | all-gather | bytes 3072 | tf_op jit(solution)/shard_map/all_gather | solution.py:17
  68.0 4.2 %all-gather.8 = f32[2,1,256]{2,1,0:T(1,128)S(1)} all-gather(f32[1,1,256]{2,1,0:T(1,128)S(1)} %bitcast.106), channel_id=3, replica_groups=mesh['pa'=16,'pb'=2] {'pb'}, dimensions={0}, use_global_device_ids=true | all-gather | bytes 3072 | tf_op jit(solution)/shard_map/all_gather | solution.py:17
  72.2 18.8 %all-gather.10 = f32[16,1,256]{2,1,0:T(1,128)S(1)} all-gather(f32[1,1,256]{2,1,0:T(1,128)S(1)} %bitcast.113), channel_id=1, replica_groups=mesh['pa'=16,'pb'=2] {'pa'}, dimensions={0}, use_global_device_ids=true | all-gather | bytes 17408 | tf_op jit(solution)/shard_map/all_gather | solution.py:131
  91.2 1.8 multiply_reduce_fusion
  93.0 11.5 %while.113 = (s32[]{:T(128)}, f32[128]{0:T(128)S(1)}, f32[128]{0:T(128)S(1)}, f32[4096]{0:T(1024)S(1)}, f32[128]{0:T(128)S(1)}, /*index=5*/f32[4096]{0:T(1024)S(...) while((s32[]{:T(128)}, f32[128]{0:T(128)S(1)}, ...), condition=%wide.region_11.0_spmd.clone, body=%wide.region_8.11_spmd.clone.sunk | while | flops 17236612 | bytes 707770 | solution.py:44
  93.2 1.1 fusion.108
  94.6 1.1 fusion.108
  96.1 1.1 fusion.108
  97.5 1.1 fusion.108
  99.0 1.1 fusion.108
  103.3 1.1 fusion.108
  104.6 17.5 %all-gather.11 = f32[16,1,128]{2,1,0:T(1,128)S(1)} all-gather(f32[1,1,128]{2,1,0:T(1,128)S(1)} %add_bitcast_fusion.1), channel_id=1, replica_groups=mesh['pa'=16,'pb'=2] {'pa'}, dimensions={0}, use_global_device_ids=true | all-gather | bytes 8704 | tf_op jit(solution)/shard_map/all_gather | solution.py:121
  122.1 2.4 %while.114 = (s32[]{:T(128)}, f32[256]{0:T(256)S(1)}, f32[256]{0:T(256)S(1)}, f32[2048]{0:T(1024)S(1)}, f32[256]{0:T(256)S(1)}, /*index=5*/f32[2048]{0:T(1024)S(...) while((s32[]{:T(128)}, f32[256]{0:T(256)S(1)}, ...), condition=%wide.region_15.0_spmd.clone, body=%wide.region_12.15_spmd.clone.sunk | while | flops 34473220 | bytes 1271994 | solution.py:44
  124.5 4.2 %all-gather.12 = f32[2,1,256]{2,1,0:T(1,128)S(1)} all-gather(f32[1,1,256]{2,1,0:T(1,128)S(1)} %bitcast.97), channel_id=4, replica_groups=mesh['pa'=16,'pb'=2] {'pb'}, dimensions={0}, use_global_device_ids=true | all-gather | bytes 3072 | tf_op jit(solution)/shard_map/all_gather | solution.py:17
  128.7 4.2 %all-gather.13 = f32[2,1,256]{2,1,0:T(1,128)S(1)} all-gather(f32[1,1,256]{2,1,0:T(1,128)S(1)} %bitcast.105), channel_id=5, replica_groups=mesh['pa'=16,'pb'=2] {'pb'}, dimensions={0}, use_global_device_ids=true | all-gather | bytes 3072 | tf_op jit(solution)/shard_map/all_gather | solution.py:17
  133.0 18.8 %all-gather.14 = f32[16,1,256]{2,1,0:T(1,128)S(1)} all-gather(f32[1,1,256]{2,1,0:T(1,128)S(1)} %bitcast.112), channel_id=1, replica_groups=mesh['pa'=16,'pb'=2] {'pa'}, dimensions={0}, use_global_device_ids=true | all-gather | bytes 17408 | tf_op jit(solution)/shard_map/all_gather | solution.py:131
  151.8 11.5 %while.115 = (s32[]{:T(128)}, f32[128]{0:T(128)S(1)}, f32[128]{0:T(128)S(1)}, f32[4096]{0:T(1024)S(1)}, f32[128]{0:T(128)S(1)}, /*index=5*/f32[4096]{0:T(1024)S(...) while((s32[]{:T(128)}, f32[128]{0:T(128)S(1)}, ...), condition=%wide.region_19.20_spmd.clone, body=%wide.region_16.19_spmd.clone.sunk | while | flops 17236612 | bytes 707770 | solution.py:44
  157.7 1.1 fusion.116
  159.2 1.1 fusion.116
  160.6 1.1 fusion.116
  163.8 17.5 %all-gather.15 = f32[16,1,128]{2,1,0:T(1,128)S(1)} all-gather(f32[1,1,128]{2,1,0:T(1,128)S(1)} %get-tuple-element.1165), channel_id=1, replica_groups=mesh['pa'=16,'pb'=2] {'pa'}, dimensions={0}, use_global_device_ids=true | all-gather | bytes 8704 | tf_op jit(solution)/shard_map/all_gather | solution.py:140
  181.3 2.4 %while.116 = (s32[]{:T(128)}, f32[256]{0:T(256)S(1)}, f32[256]{0:T(256)S(1)}, f32[2048]{0:T(1024)S(1)}, f32[256]{0:T(256)S(1)}, /*index=5*/f32[2048]{0:T(1024)S(...) while((s32[]{:T(128)}, f32[256]{0:T(256)S(1)}, ...), condition=%wide.region_23.24_spmd.clone, body=%wide.region_20.23_spmd.clone.sunk | while | flops 34473220 | bytes 1271994 | solution.py:44
  183.7 4.2 %all-gather.16 = f32[2,1,256]{2,1,0:T(1,128)S(1)} all-gather(f32[1,1,256]{2,1,0:T(1,128)S(1)} %bitcast.96), channel_id=6, replica_groups=mesh['pa'=16,'pb'=2] {'pb'}, dimensions={0}, use_global_device_ids=true | all-gather | bytes 3072 | tf_op jit(solution)/shard_map/all_gather | solution.py:17
  188.0 4.2 %all-gather.17 = f32[2,1,256]{2,1,0:T(1,128)S(1)} all-gather(f32[1,1,256]{2,1,0:T(1,128)S(1)} %bitcast.104), channel_id=7, replica_groups=mesh['pa'=16,'pb'=2] {'pb'}, dimensions={0}, use_global_device_ids=true | all-gather | bytes 3072 | tf_op jit(solution)/shard_map/all_gather | solution.py:17
  192.3 2.4 %while.117 = (s32[]{:T(128)}, f32[256,128]{1,0:T(8,128)S(1)}, f32[256]{0:T(256)S(1)}, f32[2048]{0:T(1024)S(1)}, f32[256]{0:T(256)S(1)}, /*index=5*/f32[2048]{0:T...) while((s32[]{:T(128)}, f32[256,128]{1,0:T(8,128)S(1)}, ...), condition=%wide.region_25.0_spmd.clone, body=%wide.region_24.25_spmd.clone.sunk | while | flops 67960840 | bytes 605876 | solution.py:44
  195.9 7.9 %reduce-scatter.2.cloned.1.call-done = bf16[128,128]{1,0:T(8,128)(2,1)} async-done(((bf16[256,128]{1,0:T(8,128)(2,1)}), bf16[128,128]{1,0:T(8,128)(2,1)}) %reduce-scatter.2.cloned.1.call-update) | async-done | bytes 32784 | tf_op jit(solution)/shard_map/reduce_scatter | solution.py:143
  203.8 1.4 multiply_subtract_fusion
  (242 shorter events, 25.6 us)
Async XLA Ops:
  7.2 32.3 %copy-start.3 = (f32[128]{0:T(128)S(1)}, f32[128]{0:T(128)}, u32[]{:S(2)}) copy-start(f32[128]{0:T(128)} %param.19) | copy-start | bytes 1540
  7.2 84.0 %all-gather.20.cloned.1.call-start = ((), (), s32[]{:S(2)}) async-start(), calls=%async_computation.1 | async-start | bytes 1114112 | tf_op jit(solution)/shard_map/all_gather | solution.py:112
  13.7 43.2 %copy-start = (bf16[256,128]{1,0:T(8,128)(2,1)S(1)}, bf16[256,128]{1,0:T(8,128)(2,1)}, u32[]{:S(2)}) copy-start(bf16[256,128]{1,0:T(8,128)(2,1)} %all_gather.65) | copy-start | bytes 196612
  13.7 190.1 %reduce-scatter.2.cloned.1.call-start = ((), (), s32[]{:S(2)}) async-start(), calls=%async_computation.2 | async-start | bytes 98304 | tf_op jit(solution)/shard_map/reduce_scatter | solution.py:143
  56.9 2.5 %copy-start.4 = (f32[128]{0:T(128)S(1)}, f32[128]{0:T(128)}, u32[]{:S(2)}) copy-start(f32[128]{0:T(128)} %param.18) | copy-start | bytes 1540
  56.9 34.1 %copy-start.2 = (bf16[128,128]{1,0:T(8,128)(2,1)S(1)}, bf16[128,128]{1,0:T(8,128)(2,1)}, u32[]{:S(2)}) copy-start(bf16[128,128]{1,0:T(8,128)(2,1)} %param.17) | copy-start | bytes 98308
  192.2 11.6 %copy-start.1 = (f32[128,128]{1,0:T(8,128)S(1)}, f32[128,128]{1,0:T(8,128)}, u32[]{:S(2)}) copy-start(f32[128,128]{1,0:T(8,128)} %param.16) | copy-start | bytes 196612
Sparse Core Ops, SparseCore 0:
  13.9 40.2 all-gather.19
  195.4 8.3 reduce-scatter.1
where the time goes:
time: 213 us; the launch traced here: 212 us
  blocking collectives  150 us (70%)
  matrix products  23.2 us (11%)
  between operations  14.3 us (7%)
  other arithmetic  10.3 us (5%)
  waiting for transfers between devices  8 us (4%)
  local copies, waits for them, and re-layouts  5.52 us (3%)
    all_gather x5, blocking collectives, body(): lax.all_gather(part, 'pa', axis=0, tiled=True)  90.1 us
    all_gather x6, blocking collectives, merged(): gathered = jax.tree.map(lambda a: lax.all_gather(a, axis), part)  25.4 us
    all_gather x1, blocking collectives, body(): half_targets = lax.all_gather(targets, 'pa', axis=0, tiled=True)  24.3 us
    dot_general x28, matrix products, pair_cost(): lax.dot_general(left, right, (((1,), (1,)), ((), ())), preferred_element_...  21.5 us
    reduce_scatter x1, waiting for transfers between devices, body(): lax.psum_scatter(pair_centre.astype(jnp.bfloat16), 'pb', scatter_dimensio...  7.94 us
    all_gather x1, blocking collectives, body(): pair_coarse = lax.all_gather(coarse, 'pb', axis=0, tiled=True)  5.64 us
  transfers between devices with their start and end apart: 2, of which 1 were waited for; matrix products, arithmetic and copies ran while one was open for 2% of the time, Pallas kernels for 0%

commit v1 on v0

v1 whole, which is shorter than its diff:
```python
import functools

import jax
import jax.numpy as jnp
from jax import lax
from jax.experimental import pallas as pl
from jax.experimental.pallas import tpu as pltpu
from jax.sharding import PartitionSpec as P

MESH = pl.DeviceIdType.MESH
STEP_RATE = 0.25
LOG2E = 1.4426950408889634
LN2 = 0.6931471805599453


def lse2(parts):
    high = functools.reduce(jnp.maximum, parts)
    total = functools.reduce(jnp.add, [jnp.exp2(part - high) for part in parts])
    return high + jnp.log2(total)


def spread(row, size):
    return jnp.broadcast_to(row, (size, row.shape[1])).T


def kernel(
    cores, n_pb, n_r,
    src_ref, tgt_ref, smass_ref, tmass_ref,
    moved_ref, ds_ref, dt_ref,
    rows_buf, tgt_buf, small_s, small_r, gram, acol, lane_m, lane_s, weights,
    v_own, v_in, u_own, u_in, u_sum, p_out, p_in,
    rs_send, rs_recv, ss_send, ss_recv, tg_send, tg_recv, fw_send, fw_recv,
    rb_send, rb_recv, v_send, v_recv, u_send, u_recv, p_send, p_recv,
):
    n_s = cores * n_pb
    pts = src_ref.shape[0]
    pa = lax.axis_index("pa")
    pb = lax.axis_index("pb")
    r = pa // cores
    core = lax.rem(pa, cores)
    s = core * n_pb + pb
    half = n_r // 2
    hi = r // 2
    lo = lax.rem(r, 2)

    def row_peer(k):
        other = lax.rem(s + k, n_s)
        return {"pa": r * cores + other // n_pb, "pb": lax.rem(other, n_pb)}

    def col_index(k):
        return lax.rem(r + k, n_r)

    def col_peer(k):
        return {"pa": col_index(k) * cores + core, "pb": pb}

    def by_r(index):
        return {"pa": index * cores + core, "pb": pb}

    def copy(src, dst, send, recv, where):
        return pltpu.make_async_remote_copy(
            src_ref=src, dst_ref=dst, send_sem=send, recv_sem=recv,
            device_id=where, device_id_type=MESH,
        )

    barrier = pltpu.get_barrier_semaphore()
    for k in range(1, n_r):
        pl.semaphore_signal(barrier, inc=1, device_id=col_peer(k), device_id_type=MESH)
    for k in range(1, n_s):
        pl.semaphore_signal(barrier, inc=1, device_id=row_peer(k), device_id_type=MESH)

    rows_buf[s] = src_ref[...].astype(jnp.bfloat16)
    tgt_buf[r] = tgt_ref[...]
    wide = tgt_ref[...].astype(jnp.float32)
    tnorm = jnp.sum((wide * wide).T, axis=0, keepdims=True)
    mass = tmass_ref[...]
    small_r[r] = jnp.concatenate(
        [mass * LOG2E, (mass - tnorm) * LOG2E, jnp.zeros((6, pts), jnp.float32)], axis=0
    )
    small_s[s] = jnp.broadcast_to(smass_ref[...] * LOG2E, (8, pts))

    pl.semaphore_wait(barrier, n_r - 1 + n_s - 1)

    sends = []

    def start(*args):
        item = copy(*args)
        item.start()
        sends.append(item)
        return item

    partner = r + 1 - 2 * lo
    tg = {}
    for h in range(half - 1, 0, -1):
        where = lax.rem(hi + h, half) * 2 + lo
        tg[h] = start(tgt_buf.at[r], tgt_buf.at[r], tg_send.at[h], tg_recv.at[h], by_r(where))
    row_copies = [
        start(rows_buf.at[s], rows_buf.at[s], rs_send.at[k], rs_recv.at[k], row_peer(k))
        for k in range(1, n_s)
    ]
    fw = {0: start(tgt_buf.at[r], tgt_buf.at[r], fw_send.at[0], fw_recv.at[0], by_r(partner))}
    small_r_copies = [
        start(small_r.at[r], small_r.at[r], rb_send.at[k], rb_recv.at[k], col_peer(k))
        for k in range(1, n_r)
    ]
    small_s_copies = [
        start(small_s.at[s], small_s.at[s], ss_send.at[k], ss_recv.at[k], row_peer(k))
        for k in range(1, n_s)
    ]

    def gram_block(index):
        rows = rows_buf[...].reshape(n_s * pts, rows_buf.shape[2])
        inner = lax.dot_general(
            rows, tgt_buf[index], (((1,), (1,)), ((), ())), preferred_element_type=jnp.float32
        )
        gram[index] = inner * (2.0 * LOG2E)

    for item in row_copies:
        item.wait_recv()
    gram_block(r)
    fw[0].wait_recv()
    gram_block(partner)
    for h in range(1, half):
        tg[h].wait_recv()
        origin = lax.rem(hi - h + half, half) * 2
        fw[h] = start(
            tgt_buf.at[origin + lo], tgt_buf.at[origin + lo],
            fw_send.at[h], fw_recv.at[h], by_r(partner),
        )
        gram_block(origin + lo)
    for h in range(1, half):
        fw[h].wait_recv()
        gram_block(lax.rem(hi - h + half, half) * 2 + 1 - lo)
    for item in small_r_copies:
        item.wait_recv()
    for item in small_s_copies:
        item.wait_recv()

    chunk = 64 if n_r <= 8 else 8

    def row_partial(bvec, where):
        def step(i, carry):
            at = pl.ds(pl.multiple_of(i * chunk, chunk), chunk)
            parts = [gram[b, at, :] + bvec[b] for b in range(n_r)]
            high = functools.reduce(jnp.maximum, parts)
            lane_m[at, :] = high
            lane_s[at, :] = functools.reduce(jnp.add, [jnp.exp2(p - high) for p in parts])
            return carry

        lax.fori_loop(0, n_s * pts // chunk, step, 0)
        outs = []
        for q in range(n_s):
            at = slice(q * pts, (q + 1) * pts)
            high = lane_m[at, :].T
            top = jnp.max(high, axis=0, keepdims=True)
            total = jnp.sum(lane_s[at, :].T * jnp.exp2(high - top), axis=0, keepdims=True)
            outs.append(top + jnp.log2(total))
        pad = [jnp.zeros((1, pts), jnp.float32)] * (-n_s % 8)
        v_own[where] = jnp.concatenate(outs + pad, axis=0)
        return [
            start(
                v_own.at[where], v_in.at[where, k],
                v_send.at[where, k], v_recv.at[where, k], row_peer(k),
            )
            for k in range(1, n_s)
        ]

    def row_total(copies, where):
        for item in copies:
            item.wait_recv()
        return lse2([v_own[where]] + [v_in[where, k] for k in range(1, n_s)])

    def col_update(where):
        def one(b):
            x = (gram[b] + acol[...]).reshape(n_s * pts // 8, 8, pts)
            high = jnp.max(x, axis=0)
            total = jnp.sum(jnp.exp2(x - high[None]), axis=0)
            top = jnp.max(high, axis=0, keepdims=True)
            total = jnp.sum(total * jnp.exp2(high - top), axis=0, keepdims=True)
            u_own[where, pl.ds(b, 1), :] = top + jnp.log2(total)

        def step(b, carry):
            one(b)
            return carry

        lax.fori_loop(0, n_r, step, 0)
        copies = [
            start(
                u_own.at[where], u_in.at[where, k],
                u_send.at[where, k], u_recv.at[where, k], col_peer(k),
            )
            for k in range(1, n_r)
        ]
        for item in copies:
            item.wait_recv()
        return lse2([u_own[where]] + [u_in[where, k] for k in range(1, n_r)])

    iters = u_own.shape[0]
    bvec = [small_r[b, 1:2, :] for b in range(n_r)]
    for sweep in range(iters):
        v = row_total(row_partial(bvec, sweep), sweep)
        for q in range(n_s):
            acol[q * pts : (q + 1) * pts, :] = spread(small_s[q, 0:1, :] - v[q : q + 1, :], pts)
        u = col_update(sweep)
        u_sum[...] = u
        bvec = [small_r[b, 0:1, :] - u[b : b + 1, :] for b in range(n_r)]

    v_copies = row_partial(bvec, iters)
    for q in range(n_s):
        acol[q * pts : (q + 1) * pts, :] = spread(v_own[iters, q : q + 1, :], pts)

    p_copies = {}
    own_part = None
    for k in list(range(1, n_s)) + [0]:
        q = lax.rem(s + k, n_s)
        at = pl.ds(pl.multiple_of(q * pts, pts), pts)
        base = acol[at, :]
        for b in range(n_r):
            weights[:, b * pts : (b + 1) * pts] = jnp.exp2(
                gram[b, at, :] + bvec[b] - base
            ).astype(jnp.bfloat16)
        part = jnp.dot(
            weights[...],
            tgt_buf[...].reshape(n_r * pts, tgt_buf.shape[2]),
            preferred_element_type=jnp.float32,
        )
        if k:
            p_out[k] = part.astype(jnp.bfloat16)
            p_copies[k] = start(p_out.at[k], p_in.at[k], p_send.at[k], p_recv.at[k], row_peer(k))
        else:
            own_part = part

    own_src = rows_buf[s].astype(jnp.float32)
    snorm = jnp.sum((own_src * own_src).T, axis=0, keepdims=True)
    dt_ref[...] = tnorm - LN2 * u_sum[pl.ds(r, 1), :]
    for item in v_copies:
        item.wait_recv()
    mine = [v_own[iters, pl.ds(s, 1), :]] + [
        v_in[iters, k, pl.ds(s, 1), :] for k in range(1, n_s)
    ]
    total = lse2(mine)
    ds_ref[...] = snorm - LN2 * total
    centre = spread(jnp.exp2(mine[0] - total), pts) * own_part
    for k in range(1, n_s):
        scale = spread(jnp.exp2(mine[k] - total), pts)
        p_copies[k].wait_recv()
        centre = centre + scale * p_in[k].astype(jnp.float32)
    moving = src_ref[...]
    moved_ref[...] = moving - 2.0 * STEP_RATE * (moving - centre)
    for item in sends:
        item.wait_send()


ITERS = 2


def solution(mesh):
    n_pa, n_pb = mesh.shape["pa"], mesh.shape["pb"]
    cores = 2
    n_r = n_pa // cores
    n_s = cores * n_pb

    def body(sources, targets, source_mass, target_mass):
        pts, dim = sources.shape
        rows8 = -(-n_s // 8) * 8
        dma = pltpu.SemaphoreType.DMA
        f32, bf16 = jnp.float32, jnp.bfloat16
        vmem = pl.BlockSpec(memory_space=pltpu.VMEM)
        moved, ds, dt = pl.pallas_call(
            functools.partial(kernel, cores, n_pb, n_r),
            out_shape=(
                jax.ShapeDtypeStruct((pts, dim), f32),
                jax.ShapeDtypeStruct((1, pts), f32),
                jax.ShapeDtypeStruct((1, pts), f32),
            ),
            in_specs=[vmem] * 4,
            out_specs=(vmem,) * 3,
            scratch_shapes=[
                pltpu.VMEM((n_s, pts, dim), bf16),
                pltpu.VMEM((n_r, pts, dim), bf16),
                pltpu.VMEM((n_s, 8, pts), f32),
                pltpu.VMEM((n_r, 8, pts), f32),
                pltpu.VMEM((n_r, n_s * pts, pts), f32),
                pltpu.VMEM((n_s * pts, pts), f32),
                pltpu.VMEM((n_s * pts, pts), f32),
                pltpu.VMEM((n_s * pts, pts), f32),
                pltpu.VMEM((pts, n_r * pts), bf16),
                pltpu.VMEM((ITERS + 1, rows8, pts), f32),
                pltpu.VMEM((ITERS + 1, n_s, rows8, pts), f32),
                pltpu.VMEM((ITERS, n_r, pts), f32),
                pltpu.VMEM((ITERS, n_r, n_r, pts), f32),
                pltpu.VMEM((n_r, pts), f32),
                pltpu.VMEM((n_s, pts, dim), bf16),
                pltpu.VMEM((n_s, pts, dim), bf16),
                dma((n_s,)), dma((n_s,)), dma((n_s,)), dma((n_s,)),
                dma((n_r,)), dma((n_r,)), dma((n_r,)), dma((n_r,)),
                dma((n_r,)), dma((n_r,)),
                dma((ITERS + 1, n_s)), dma((ITERS + 1, n_s)),
                dma((ITERS, n_r)), dma((ITERS, n_r)),
                dma((n_s,)), dma((n_s,)),
            ],
            compiler_params=pltpu.CompilerParams(
                collective_id=0, has_side_effects=True, vmem_limit_bytes=60 * 1024 * 1024
            ),
        )(sources, targets, source_mass[None, :], target_mass[None, :])
        return moved, ds[0], dt[0]

    return jax.shard_map(
        body,
        mesh=mesh,
        in_specs=(P(("pa", "pb"), None), P(("pa", "pb"), None), P(("pa", "pb")), P(("pa", "pb"))),
        out_specs=(P(("pa", "pb"), None), P(("pa", "pb")), P(("pa", "pb"))),
        check_vma=False,
    )
```

time: 213 us -> 42 us (0.20)
  blocking collectives: 150 us -> 0 us
  Pallas kernels: 0 us -> 38.5 us
  matrix products: 23.2 us -> 0 us
  between operations: 14.3 us -> 0.65 us
  other arithmetic: 10.3 us -> 0 us
  waiting for transfers between devices: 8 us -> 0 us
  local copies, waits for them, and re-layouts: 5.52 us -> 2.59 us
    all_gather x14 -> x0, blocking collectives: 150 us -> none  [the longest x5 90.1 us: body(): lax.all_gather(part, 'pa', axis=0, tiled=True)]
    pallas_call x0 -> x1, Pallas kernels: none -> 38.5 us  [body(): pl.pallas_call(functools.partial(kernel, cores, n_pb, n_r), out_shape=(ja...]
    dot_general x32 -> x0, matrix products: 23.2 us -> none  [the longest x28 21.5 us: pair_cost(): lax.dot_general(left, right, (((1,), (1,)), ((), ())), preferred_element_...]
    reduce_scatter x1 -> x0, waiting for transfers between devices: 7.94 us -> none  [body(): lax.psum_scatter(pair_centre.astype(jnp.bfloat16), 'pb', scatter_dimensio...]
    reduce_sum x32 -> x0, other arithmetic: 6.21 us -> none  [the longest x4 3.24 us: squares(): return jnp.sum(wide * wide, axis=1)]
    dynamic_slice x71 -> x0, local copies, waits for them, and re-layouts: 5.46 us -> none  [the longest x32 2.48 us: update(): lax.dynamic_slice_in_dim(column_norm, start + offset, length, 0)]
    unnamed x10 -> x7, local copies, waits for them, and re-layouts: 0.02 us -> 2.59 us
  transfers between devices with their start and end apart: 2 -> 0, of which waited for: 1 -> 0; matrix products, arithmetic and copies ran while one was open for 2% -> 0% of each run, Pallas kernels for 0% -> 0%
where the time goes in v1:
time: 42 us; the launch traced here: 41.8 us
  Pallas kernels  38.5 us (92%)
  local copies, waits for them, and re-layouts  2.59 us (6%)
  between operations  0.65 us (2%)
    pallas_call x1, Pallas kernels, body(): pl.pallas_call(functools.partial(kernel, cores, n_pb, n_r), out_shape=(ja...  38.5 us
    unnamed x7, local copies, waits for them, and re-layouts  2.59 us

profile of v1, /device:TPU:0, one launch (start us, length us, event | category | flops | bytes accessed | tf_op | source)
XLA Modules:
  0.0 41.8 jit_solution(15457321292798412982)
XLA Ops:
  0.6 38.5 %shard_map.67 = (f32[128,128]{1,0:T(8,128)}, f32[1,128]{1,0:T(1,128)}, f32[1,128]{1,0:T(1,128)}) custom-call(f32[128,128]{1,0:T(8,128)} %src_ref.1, bf16[128,128]{1,0:T(8,128)(2,1)} %tgt_ref.1, f32[1,128]{1,0:T(1,128)} %bitcast.4, f32[1,128]{1,0:T(1,128)} %bitcast.5), custom_call_target="tpu_custom_call" | custom-call | tf_op jit(solution)/shard_map/pallas_call | solution.py:268
  39.2 0.0 copy-start.1
  39.2 1.5 %copy.10 = f32[128,128]{1,0:T(8,128)} copy(f32[128,128]{1,0:T(8,128)} %get-tuple-element.12) | data formatting | bytes 131072
  40.6 0.0 copy-done.1
  40.6 0.0 copy-start
  40.6 0.5 %copy.11 = f32[128]{0:T(128)} copy(f32[128]{0:T(128)S(1)} %bitcast.7) | data formatting | bytes 1024
  41.2 0.1 copy-done
  41.2 0.5 %copy.12 = f32[128]{0:T(128)} copy(f32[128]{0:T(128)S(1)} %bitcast.6) | data formatting | bytes 1024
Async XLA Ops:
  39.2 1.5 %copy-start.1 = (f32[1,128]{1,0:T(1,128)S(1)}, f32[1,128]{1,0:T(1,128)}, u32[]{:S(2)}) copy-start(f32[1,128]{1,0:T(1,128)} %get-tuple-element.7) | copy-start | bytes 1540
  40.6 0.6 %copy-start = (f32[1,128]{1,0:T(1,128)S(1)}, f32[1,128]{1,0:T(1,128)}, u32[]{:S(2)}) copy-start(f32[1,128]{1,0:T(1,128)} %get-tuple-element.8) | copy-start | bytes 1540

commit v2 on v1

--- a/solution.py
+++ b/solution.py
@@ -11,6 +11,7 @@
 STEP_RATE = 0.25
 LOG2E = 1.4426950408889634
 LN2 = 0.6931471805599453
+EXTRA = 16
 
 
 def lse2(parts):
@@ -23,17 +24,54 @@
     return jnp.broadcast_to(row, (size, row.shape[1])).T
 
 
+def pack_rows(rows):
+    pieces = []
+    for row in rows:
+        for _ in range(3):
+            part = row.astype(jnp.bfloat16).astype(jnp.float32)
+            pieces.append(part)
+            row = row - part
+    pad = jnp.zeros((EXTRA - len(pieces), rows[0].shape[1]), jnp.float32)
+    return jnp.concatenate(pieces + [pad], axis=0).astype(jnp.bfloat16)
+
+
+def unpack_row(buf, index, start, which):
+    rows = buf[index, start:, :].astype(jnp.float32)
+    at = 3 * which
+    return rows[at : at + 1] + rows[at + 1 : at + 2] + rows[at + 2 : at + 3]
+
+
+def finish(moved_in, ds_in, dt_in, moved_ref, ds_ref, dt_ref):
+    moved_ref[...] = moved_in[...]
+    ds_ref[...] = ds_in[...]
+    dt_ref[...] = dt_in[...]
+
+
+def repeat(count, unrolled, step):
+    if unrolled:
+        for i in range(count):
+            step(i, 0)
+    else:
+        lax.fori_loop(0, count, step, 0)
+
+
 def kernel(
     cores, n_pb, n_r,
-    src_ref, tgt_ref, smass_ref, tmass_ref,
+    src_hbm, tgt_hbm, smass_hbm, tmass_hbm,
     moved_ref, ds_ref, dt_ref,
-    rows_buf, tgt_buf, small_s, small_r, gram, acol, lane_m, lane_s, weights,
+    src_ref, tgt_ref, smass_ref, tmass_ref, load_sem,
+    rows_pk, tgt_pk, rows_buf, tgt_buf, gram, acol, lane_m, lane_s, weights,
     v_own, v_in, u_own, u_in, u_sum, p_out, p_in,
-    rs_send, rs_recv, ss_send, ss_recv, tg_send, tg_recv, fw_send, fw_recv,
-    rb_send, rb_recv, v_send, v_recv, u_send, u_recv, p_send, p_recv,
+    rs_send, rs_recv, tg_send, tg_recv, fw_send, fw_recv, v_send, v_recv, u_send, u_recv, p_send, p_recv,
 ):
     n_s = cores * n_pb
     pts = src_ref.shape[0]
+    loads = [
+        pltpu.make_async_copy(a, b, load_sem.at[i])
+        for i, (a, b) in enumerate(
+            [(tgt_hbm, tgt_ref), (tmass_hbm, tmass_ref), (src_hbm, src_ref), (smass_hbm, smass_ref)]
+        )
+    ]
     pa = lax.axis_index("pa")
     pb = lax.axis_index("pb")
     r = pa // cores
@@ -62,23 +100,30 @@
             device_id=where, device_id_type=MESH,
         )
 
+    partner = r + 1 - 2 * lo
+
+    def line(h):
+        return lax.rem(hi + h, half) * 2 + lo
+
     barrier = pltpu.get_barrier_semaphore()
-    for k in range(1, n_r):
-        pl.semaphore_signal(barrier, inc=1, device_id=col_peer(k), device_id_type=MESH)
-    for k in range(1, n_s):
-        pl.semaphore_signal(barrier, inc=1, device_id=row_peer(k), device_id_type=MESH)
-
-    rows_buf[s] = src_ref[...].astype(jnp.bfloat16)
-    tgt_buf[r] = tgt_ref[...]
+    peers = [by_r(line(h)) for h in range(1, half)] + [by_r(partner)]
+    peers += [row_peer(k) for k in range(1, n_s)]
+    for where in peers:
+        pl.semaphore_signal(barrier, inc=1, device_id=where, device_id_type=MESH)
+    for item in loads:
+        item.start()
+    for item in loads:
+        item.wait()
+
+    tgt_pk[r, :pts, :] = tgt_ref[...]
     wide = tgt_ref[...].astype(jnp.float32)
     tnorm = jnp.sum((wide * wide).T, axis=0, keepdims=True)
     mass = tmass_ref[...]
-    small_r[r] = jnp.concatenate(
-        [mass * LOG2E, (mass - tnorm) * LOG2E, jnp.zeros((6, pts), jnp.float32)], axis=0
-    )
-    small_s[s] = jnp.broadcast_to(smass_ref[...] * LOG2E, (8, pts))
-
-    pl.semaphore_wait(barrier, n_r - 1 + n_s - 1)
+    tgt_pk[r, pts:, :] = pack_rows([mass * LOG2E, (mass - tnorm) * LOG2E])
+    rows_pk[s, :pts, :] = src_ref[...].astype(jnp.bfloat16)
+    rows_pk[s, pts:, :] = pack_rows([smass_ref[...] * LOG2E])
+
+    pl.semaphore_wait(barrier, len(peers))
 
     sends = []
 
@@ -88,65 +133,57 @@
         sends.append(item)
         return item
 
-    partner = r + 1 - 2 * lo
-    tg = {}
-    for h in range(half - 1, 0, -1):
-        where = lax.rem(hi + h, half) * 2 + lo
-        tg[h] = start(tgt_buf.at[r], tgt_buf.at[r], tg_send.at[h], tg_recv.at[h], by_r(where))
+    along = {
+        h: start(
+            tgt_pk.at[r], tgt_pk.at[r], tg_send.at[h], tg_recv.at[h], by_r(line(h))
+        )
+        for h in range(1, half)
+    }
+    across = {
+        0: start(tgt_pk.at[r], tgt_pk.at[r], fw_send.at[0], fw_recv.at[0], by_r(partner))
+    }
     row_copies = [
-        start(rows_buf.at[s], rows_buf.at[s], rs_send.at[k], rs_recv.at[k], row_peer(k))
+        start(rows_pk.at[s], rows_pk.at[s], rs_send.at[k], rs_recv.at[k], row_peer(k))
         for k in range(1, n_s)
     ]
-    fw = {0: start(tgt_buf.at[r], tgt_buf.at[r], fw_send.at[0], fw_recv.at[0], by_r(partner))}
-    small_r_copies = [
-        start(small_r.at[r], small_r.at[r], rb_send.at[k], rb_recv.at[k], col_peer(k))
-        for k in range(1, n_r)
-    ]
-    small_s_copies = [
-        start(small_s.at[s], small_s.at[s], ss_send.at[k], ss_recv.at[k], row_peer(k))
-        for k in range(1, n_s)
-    ]
 
     def gram_block(index):
-        rows = rows_buf[...].reshape(n_s * pts, rows_buf.shape[2])
         inner = lax.dot_general(
-            rows, tgt_buf[index], (((1,), (1,)), ((), ())), preferred_element_type=jnp.float32
+            rows_buf[...], tgt_pk[index, :pts, :], (((1,), (1,)), ((), ())),
+            preferred_element_type=jnp.float32,
         )
         gram[index] = inner * (2.0 * LOG2E)
+        tgt_buf[index] = tgt_pk[index, :pts, :]
 
     for item in row_copies:
         item.wait_recv()
+    for q in range(n_s):
+        rows_buf[q * pts : (q + 1) * pts, :] = rows_pk[q, :pts, :]
     gram_block(r)
-    fw[0].wait_recv()
-    gram_block(partner)
     for h in range(1, half):
-        tg[h].wait_recv()
-        origin = lax.rem(hi - h + half, half) * 2
-        fw[h] = start(
-            tgt_buf.at[origin + lo], tgt_buf.at[origin + lo],
-            fw_send.at[h], fw_recv.at[h], by_r(partner),
-        )
-        gram_block(origin + lo)
-    for h in range(1, half):
-        fw[h].wait_recv()
-        gram_block(lax.rem(hi - h + half, half) * 2 + 1 - lo)
-    for item in small_r_copies:
-        item.wait_recv()
-    for item in small_s_copies:
-        item.wait_recv()
-
-    chunk = 64 if n_r <= 8 else 8
+        along[h].wait_recv()
+        block = line(half - h)
+        across[h] = start(
+            tgt_pk.at[block], tgt_pk.at[block], fw_send.at[h], fw_recv.at[h], by_r(partner)
+        )
+        gram_block(block)
+    for h in range(half):
+        across[h].wait_recv()
+        gram_block(line(half - h) + 1 - 2 * lo)
+
+    chunk = 16
 
     def row_partial(bvec, where):
         def step(i, carry):
-            at = pl.ds(pl.multiple_of(i * chunk, chunk), chunk)
+            first = i * chunk if isinstance(i, int) else pl.multiple_of(i * chunk, chunk)
+            at = pl.ds(first, chunk)
             parts = [gram[b, at, :] + bvec[b] for b in range(n_r)]
             high = functools.reduce(jnp.maximum, parts)
             lane_m[at, :] = high
             lane_s[at, :] = functools.reduce(jnp.add, [jnp.exp2(p - high) for p in parts])
             return carry
 
-        lax.fori_loop(0, n_s * pts // chunk, step, 0)
+        repeat(n_s * pts // chunk, n_r <= 8, step)
         outs = []
         for q in range(n_s):
             at = slice(q * pts, (q + 1) * pts)
@@ -182,7 +219,7 @@
             one(b)
             return carry
 
-        lax.fori_loop(0, n_r, step, 0)
+        repeat(n_r, n_r <= 8, step)
         copies = [
             start(
                 u_own.at[where], u_in.at[where, k],
@@ -195,14 +232,14 @@
         return lse2([u_own[where]] + [u_in[where, k] for k in range(1, n_r)])
 
     iters = u_own.shape[0]
-    bvec = [small_r[b, 1:2, :] for b in range(n_r)]
+    bvec = [unpack_row(tgt_pk, b, pts, 1) for b in range(n_r)]
     for sweep in range(iters):
         v = row_total(row_partial(bvec, sweep), sweep)
         for q in range(n_s):
-            acol[q * pts : (q + 1) * pts, :] = spread(small_s[q, 0:1, :] - v[q : q + 1, :], pts)
+            acol[q * pts : (q + 1) * pts, :] = spread(unpack_row(rows_pk, q, pts, 0) - v[q : q + 1, :], pts)
         u = col_update(sweep)
         u_sum[...] = u
-        bvec = [small_r[b, 0:1, :] - u[b : b + 1, :] for b in range(n_r)]
+        bvec = [unpack_row(tgt_pk, b, pts, 0) - u[b : b + 1, :] for b in range(n_r)]
 
     v_copies = row_partial(bvec, iters)
     for q in range(n_s):
@@ -229,7 +266,7 @@
         else:
             own_part = part
 
-    own_src = rows_buf[s].astype(jnp.float32)
+    own_src = rows_pk[s, :pts, :].astype(jnp.float32)
     snorm = jnp.sum((own_src * own_src).T, axis=0, keepdims=True)
     dt_ref[...] = tnorm - LN2 * u_sum[pl.ds(r, 1), :]
     for item in v_copies:
@@ -265,20 +302,26 @@
         dma = pltpu.SemaphoreType.DMA
         f32, bf16 = jnp.float32, jnp.bfloat16
         vmem = pl.BlockSpec(memory_space=pltpu.VMEM)
-        moved, ds, dt = pl.pallas_call(
+        results = (
+            jax.ShapeDtypeStruct((pts, dim), f32),
+            jax.ShapeDtypeStruct((1, pts), f32),
+            jax.ShapeDtypeStruct((1, pts), f32),
+        )
+        parts = pl.pallas_call(
             functools.partial(kernel, cores, n_pb, n_r),
-            out_shape=(
-                jax.ShapeDtypeStruct((pts, dim), f32),
-                jax.ShapeDtypeStruct((1, pts), f32),
-                jax.ShapeDtypeStruct((1, pts), f32),
-            ),
-            in_specs=[vmem] * 4,
+            out_shape=results,
+            in_specs=[pl.BlockSpec(memory_space=pl.ANY)] * 4,
             out_specs=(vmem,) * 3,
             scratch_shapes=[
-                pltpu.VMEM((n_s, pts, dim), bf16),
+                pltpu.VMEM((pts, dim), f32),
+                pltpu.VMEM((pts, dim), bf16),
+                pltpu.VMEM((1, pts), f32),
+                pltpu.VMEM((1, pts), f32),
+                dma((4,)),
+                pltpu.VMEM((n_s, pts + EXTRA, dim), bf16),
+                pltpu.VMEM((n_r, pts + EXTRA, dim), bf16),
+                pltpu.VMEM((n_s * pts, dim), bf16),
                 pltpu.VMEM((n_r, pts, dim), bf16),
-                pltpu.VMEM((n_s, 8, pts), f32),
-                pltpu.VMEM((n_r, 8, pts), f32),
                 pltpu.VMEM((n_r, n_s * pts, pts), f32),
                 pltpu.VMEM((n_s * pts, pts), f32),
                 pltpu.VMEM((n_s * pts, pts), f32),
@@ -291,9 +334,8 @@
                 pltpu.VMEM((n_r, pts), f32),
                 pltpu.VMEM((n_s, pts, dim), bf16),
                 pltpu.VMEM((n_s, pts, dim), bf16),
-                dma((n_s,)), dma((n_s,)), dma((n_s,)), dma((n_s,)),
+                dma((n_s,)), dma((n_s,)),
                 dma((n_r,)), dma((n_r,)), dma((n_r,)), dma((n_r,)),
-                dma((n_r,)), dma((n_r,)),
                 dma((ITERS + 1, n_s)), dma((ITERS + 1, n_s)),
                 dma((ITERS, n_r)), dma((ITERS, n_r)),
                 dma((n_s,)), dma((n_s,)),
@@ -302,6 +344,9 @@
                 collective_id=0, has_side_effects=True, vmem_limit_bytes=60 * 1024 * 1024
             ),
         )(sources, targets, source_mass[None, :], target_mass[None, :])
+        moved, ds, dt = pl.pallas_call(
+            finish, out_shape=results, in_specs=[vmem] * 3, out_specs=(vmem,) * 3
+        )(*parts)
         return moved, ds[0], dt[0]
 
     return jax.shard_map(

time: 42 us -> 37.6 us (0.90)
  local copies, waits for them, and re-layouts: 2.59 us -> 0 us
  Pallas kernels: 38.5 us -> 36.8 us
    unnamed x7 -> x0, local copies, waits for them, and re-layouts: 2.59 us -> none
    pallas_call x1 -> x2, Pallas kernels: 38.5 us -> 36.8 us  [the longest x1 35.3 us: body(): pl.pallas_call(functools.partial(kernel, cores, n_pb, n_r), out_shape=res...]
where the time goes in v2:
time: 37.6 us; the launch traced here: 37.4 us
  Pallas kernels  36.8 us (98%)
  between operations  0.64 us (2%)
    pallas_call x1, Pallas kernels, body(): pl.pallas_call(functools.partial(kernel, cores, n_pb, n_r), out_shape=res...  35.3 us
    pallas_call x1, Pallas kernels, body(): pl.pallas_call(finish, out_shape=results, in_specs=[vmem] * 3, out_specs=...  1.48 us

profile of v2, /device:TPU:0, one launch (start us, length us, event | category | flops | bytes accessed | tf_op | source)
XLA Modules:
  0.0 37.4 jit_solution(9284991707448182526)
XLA Ops:
  0.6 35.3 %shard_map.67 = (f32[128,128]{1,0:T(8,128)}, f32[1,128]{1,0:T(1,128)}, f32[1,128]{1,0:T(1,128)}) custom-call(f32[128,128]{1,0:T(8,128)} %src_hbm.1, bf16[128,128]{1,0:T(8,128)(2,1)} %tgt_hbm.1, f32[1,128]{1,0:T(1,128)} %bitcast.4, f32[1,128]{1,0:T(1,128)} %bitcast.5), custom_call_target="tpu_custom_call" | custom-call | tf_op jit(solution)/shard_map/pallas_call | solution.py:310
  35.9 1.5 %shard_map.68 = (f32[128,128]{1,0:T(8,128)}, f32[1,128]{1,0:T(1,128)}, f32[1,128]{1,0:T(1,128)}) custom-call(f32[128,128]{1,0:T(8,128)} %get-tuple-element.9.moved_in, f32[1,128]{1,0:T(1,128)} %get-tuple-element.10.ds_in, f32[1,128]{1,0:T(1,128)} %get-tuple-element.11.dt_in), custom_call_target="tpu_custom_call" | custom-call | tf_op jit(solution)/shard_map/pallas_call | solution.py:347

commit v3 on v2

--- a/solution.py
+++ b/solution.py
@@ -102,11 +102,15 @@
 
     partner = r + 1 - 2 * lo
 
-    def line(h):
-        return lax.rem(hi + h, half) * 2 + lo
+    near = jnp.minimum(hi, half - 1 - hi)
+    outer = jnp.where(hi > half - 1 - hi, -1, 1)
+
+    def line(j):
+        both = (j + 1) // 2 * (1 if j % 2 else -1)
+        return (hi + jnp.where(j <= 2 * near, both, outer * (j - near))) * 2 + lo
 
     barrier = pltpu.get_barrier_semaphore()
-    peers = [by_r(line(h)) for h in range(1, half)] + [by_r(partner)]
+    peers = [by_r(line(j)) for j in range(1, half)] + [by_r(partner)]
     peers += [row_peer(k) for k in range(1, n_s)]
     for where in peers:
         pl.semaphore_signal(barrier, inc=1, device_id=where, device_id_type=MESH)
@@ -133,12 +137,8 @@
         sends.append(item)
         return item
 
-    along = {
-        h: start(
-            tgt_pk.at[r], tgt_pk.at[r], tg_send.at[h], tg_recv.at[h], by_r(line(h))
-        )
-        for h in range(1, half)
-    }
+    for j in range(half - 1, 0, -1):
+        start(tgt_pk.at[r], tgt_pk.at[r], tg_send.at[j], tg_recv.at[r], by_r(line(j)))
     across = {
         0: start(tgt_pk.at[r], tgt_pk.at[r], fw_send.at[0], fw_recv.at[0], by_r(partner))
     }
@@ -160,16 +160,15 @@
     for q in range(n_s):
         rows_buf[q * pts : (q + 1) * pts, :] = rows_pk[q, :pts, :]
     gram_block(r)
-    for h in range(1, half):
-        along[h].wait_recv()
-        block = line(half - h)
-        across[h] = start(
-            tgt_pk.at[block], tgt_pk.at[block], fw_send.at[h], fw_recv.at[h], by_r(partner)
-        )
+    for j in range(1, half):
+        block = line(j)
+        landed = tgt_pk.at[block]
+        copy(landed, landed, tg_send.at[j], tg_recv.at[block], by_r(block)).wait_recv()
+        across[j] = start(landed, landed, fw_send.at[j], fw_recv.at[j], by_r(partner))
         gram_block(block)
-    for h in range(half):
-        across[h].wait_recv()
-        gram_block(line(half - h) + 1 - 2 * lo)
+    for j in range(half):
+        across[j].wait_recv()
+        gram_block(line(j) + 1 - 2 * lo)
 
     chunk = 16
 
@@ -220,16 +219,20 @@
             return carry
 
         repeat(n_r, n_r <= 8, step)
-        copies = [
+        for at, index in enumerate(
+            [line(j) + flip for j in range(half - 1, -1, -1) for flip in (1 - 2 * lo, 0)][:-1]
+        ):
             start(
-                u_own.at[where], u_in.at[where, k],
-                u_send.at[where, k], u_recv.at[where, k], col_peer(k),
+                u_own.at[where], u_in.at[where, r],
+                u_send.at[where, at], u_recv.at[where, r], by_r(index),
             )
-            for k in range(1, n_r)
-        ]
-        for item in copies:
-            item.wait_recv()
-        return lse2([u_own[where]] + [u_in[where, k] for k in range(1, n_r)])
+        others = [lax.rem(r + k, n_r) for k in range(1, n_r)]
+        for index in others:
+            landed = u_in.at[where, index]
+            copy(
+                u_own.at[where], landed, u_send.at[where, 0], u_recv.at[where, index], by_r(index)
+            ).wait_recv()
+        return lse2([u_own[where]] + [u_in[where, index] for index in others])
 
     iters = u_own.shape[0]
     bvec = [unpack_row(tgt_pk, b, pts, 1) for b in range(n_r)]
@@ -247,16 +250,16 @@
 
     p_copies = {}
     own_part = None
-    for k in list(range(1, n_s)) + [0]:
+    for k in sorted(range(1, n_s), key=lambda k: k % n_pb == 0) + [0]:
         q = lax.rem(s + k, n_s)
         at = pl.ds(pl.multiple_of(q * pts, pts), pts)
         base = acol[at, :]
         for b in range(n_r):
-            weights[:, b * pts : (b + 1) * pts] = jnp.exp2(
+            weights[k, :, b * pts : (b + 1) * pts] = jnp.exp2(
                 gram[b, at, :] + bvec[b] - base
             ).astype(jnp.bfloat16)
         part = jnp.dot(
-            weights[...],
+            weights[k],
             tgt_buf[...].reshape(n_r * pts, tgt_buf.shape[2]),
             preferred_element_type=jnp.float32,
         )
@@ -326,7 +329,7 @@
                 pltpu.VMEM((n_s * pts, pts), f32),
                 pltpu.VMEM((n_s * pts, pts), f32),
                 pltpu.VMEM((n_s * pts, pts), f32),
-                pltpu.VMEM((pts, n_r * pts), bf16),
+                pltpu.VMEM((n_s, pts, n_r * pts), bf16),
                 pltpu.VMEM((ITERS + 1, rows8, pts), f32),
                 pltpu.VMEM((ITERS + 1, n_s, rows8, pts), f32),
                 pltpu.VMEM((ITERS, n_r, pts), f32),

time: 37.6 us -> 37.3 us (level)
  Pallas kernels: 36.8 us -> 36.4 us
where the time goes in v3:
time: 37.3 us; the launch traced here: 37.1 us
  Pallas kernels  36.4 us (98%)
  between operations  0.64 us (2%)
    pallas_call x1, Pallas kernels, body(): pl.pallas_call(functools.partial(kernel, cores, n_pb, n_r), out_shape=res...  34.9 us
    pallas_call x1, Pallas kernels, body(): pl.pallas_call(finish, out_shape=results, in_specs=[vmem] * 3, out_specs=...  1.48 us

profile of v3, /device:TPU:0, one launch (start us, length us, event | category | flops | bytes accessed | tf_op | source)
XLA Modules:
  0.0 37.1 jit_solution(874831413876595300)
XLA Ops:
  0.6 34.9 %shard_map.67 = (f32[128,128]{1,0:T(8,128)}, f32[1,128]{1,0:T(1,128)}, f32[1,128]{1,0:T(1,128)}) custom-call(f32[128,128]{1,0:T(8,128)} %src_hbm.1, bf16[128,128]{1,0:T(8,128)(2,1)} %tgt_hbm.1, f32[1,128]{1,0:T(1,128)} %bitcast.4, f32[1,128]{1,0:T(1,128)} %bitcast.5), custom_call_target="tpu_custom_call" | custom-call | tf_op jit(solution)/shard_map/pallas_call | solution.py:313
  35.6 1.5 %shard_map.68 = (f32[128,128]{1,0:T(8,128)}, f32[1,128]{1,0:T(1,128)}, f32[1,128]{1,0:T(1,128)}) custom-call(f32[128,128]{1,0:T(8,128)} %get-tuple-element.9.moved_in, f32[1,128]{1,0:T(1,128)} %get-tuple-element.10.ds_in, f32[1,128]{1,0:T(1,128)} %get-tuple-element.11.dt_in), custom_call_target="tpu_custom_call" | custom-call | tf_op jit(solution)/shard_map/pallas_call | solution.py:350
